TPU v7x, 256 devices: a whole 4x4x8 slice. The times are simulated.
256 devices in a mesh: replica: 16 (over z_lo, y, core), model: 16 (over z_hi, x).
Axes of the slice: x: 4, y: 4, z: 8 (z_hi: 4, z_lo: 2; z = z_hi * 2 + z_lo), core: 2. Of those that a mesh axis runs over, the one named last changes fastest.
Arguments:
- partial_query: float32 [16, 2048, 2048], P('replica', None, 'model'), may hold values from -4 to 4
- partial_key: float32 [16, 2048, 2048], P('replica', None, 'model'), may hold values from -4 to 4
- partial_value: float32 [16, 2048, 2048], P('replica', None, 'model'), may hold values from -4 to 4
- partial_mixed: float32 [16, 2048, 2048], P('replica', 'model'), may hold values from -4 to 4
- partial_norm: float32 [16, 2048], P('replica'), may hold values from -8 to 8
- partial_bias: float32 [16, 2048], P('replica'), may hold values from -8 to 8
- master_query: float32 [2048, 2048], P('replica', 'model'), may hold values from -0.1875 to 0.1875
- master_key: float32 [2048, 2048], P('replica', 'model'), may hold values from -0.1875 to 0.1875
- master_value: float32 [2048, 2048], P('replica', 'model'), may hold values from -0.1875 to 0.1875
- master_mixed: float32 [2048, 2048], P('model', 'replica'), may hold values from -0.1875 to 0.1875
- master_norm: float32 [2048], P('replica'), may hold values from 0.25 to 1.75
- master_bias: float32 [2048], P('replica'), may hold values from -3 to 3
- memory_query: float32 [2048, 2048], P('replica', 'model'), may hold values from 9.765625e-05 to 0.0009765625
- memory_key: float32 [2048, 2048], P('replica', 'model'), may hold values from 9.765625e-05 to 0.0009765625
- memory_value: float32 [2048, 2048], P('replica', 'model'), may hold values from 9.765625e-05 to 0.0009765625
- memory_mixed: float32 [2048, 2048], P('model', 'replica'), may hold values from 9.765625e-05 to 0.0009765625
- memory_norm: float32 [2048], P('replica'), may hold values from 0.05 to 0.8
- memory_bias: float32 [2048], P('replica'), may hold values from 0.05 to 0.8
Outputs:
- compute_query: bfloat16 [2048, 2048], P(None, 'model')
- compute_key: bfloat16 [2048, 2048], P(None, 'model')
- compute_value: bfloat16 [2048, 2048], P(None, 'model')
- compute_mixed: bfloat16 [2048, 2048], P('model')
- compute_norm: bfloat16 [2048], replicated
- compute_bias: bfloat16 [2048], replicated
- stepped_query: float32 [2048, 2048], P('replica', 'model')
- stepped_key: float32 [2048, 2048], P('replica', 'model')
- stepped_value: float32 [2048, 2048], P('replica', 'model')
- stepped_mixed: float32 [2048, 2048], P('model', 'replica')
- stepped_norm: float32 [2048], P('replica')
- stepped_bias: float32 [2048], P('replica')
- state_new_query: float32 [2048, 2048], P('replica', 'model')
- state_new_key: float32 [2048, 2048], P('replica', 'model')
- state_new_value: float32 [2048, 2048], P('replica', 'model')
- state_new_mixed: float32 [2048, 2048], P('model', 'replica')
- state_new_norm: float32 [2048], P('replica')
- state_new_bias: float32 [2048], P('replica')
All inputs are finite; a program needn't handle non-finite values.
Results may differ from a plain program's by a relative error of at most 0.0004.
Values may be sent and summed in bfloat16 or wider, within the bound.
A program may use at most 64 MiB of HBM per device.

v0:
```python
import jax
import jax.numpy as jnp
from jax import lax
from jax.sharding import Mesh
from jax.sharding import PartitionSpec as P

REPLICA = ("replica_0", "replica_1", "replica_2")
learn_rate = 0.015
hold_rate = 0.8


def cut_along(x, dim, size):
    before, after = (x.shape[:dim], x.shape[dim + 1 :])
    return jnp.moveaxis(x.reshape(*before, size, -1, *after), dim, 0)


def sum_at_owner(x, axis, dim):
    size = lax.axis_size(axis)
    blocks = lax.all_to_all(cut_along(x, dim, size), axis, 0, 0, tiled=True)
    return jnp.sum(blocks, axis=0)


def sum_by_axis(x, axes, dim):
    far, near = axes
    own = sum_at_owner(cut_along(x, dim, lax.axis_size(far)), near, dim + 1)
    return jnp.sum(lax.all_to_all(own, far, 0, 0, tiled=True), axis=0)


def in_one_piece(arrays, axis, dim, along):
    widths = [a.shape[along] for a in arrays]
    both = jnp.concatenate(arrays, axis=along)
    out = sum_by_axis(both, axis, dim)
    return tuple(jnp.split(out, [sum(widths[:k]) for k in range(1, len(widths))], axis=along))


def copy_for_each(x, axis):
    copies = jnp.broadcast_to(x, (lax.axis_size(axis), *x.shape))
    return lax.all_to_all(copies, axis, split_axis=0, concat_axis=0, tiled=True)


def of_everyone(x, axis):
    return copy_for_each(x, axis).sum(axis=0)


def together(arrays, axis):
    ends = [0]
    for a in arrays:
        ends.append(ends[-1] + a.size)
    subtotal = of_everyone(jnp.concatenate([a.ravel() for a in arrays]), axis)
    return tuple((subtotal[b:e].reshape(a.shape) for a, b, e in zip(arrays, ends, ends[1:])))


def gather_turned(arrays, axis, dims):
    turned = [jnp.moveaxis(a, dim, 0) for a, dim in zip(arrays, dims)]
    both = jnp.concatenate([t.reshape(len(t), -1) for t in turned], axis=1)
    out, at, outs = (lax.all_gather(both, axis, axis=0, tiled=True), 0, [])
    for t, dim in zip(turned, dims):
        share = out[:, at : at + t[0].size].reshape(-1, *t.shape[1:])
        outs.append(jnp.moveaxis(share, 0, dim))
        at += t[0].size
    return tuple(outs)


def shards(
    partial_query,
    partial_key,
    partial_value,
    partial_mixed,
    partial_norm,
    partial_bias,
    master_query,
    master_key,
    master_value,
    master_mixed,
    master_norm,
    master_bias,
    memory_query,
    memory_key,
    memory_value,
    memory_mixed,
    memory_norm,
    memory_bias,
):
    mean_query, mean_key, mean_value, mean_mixed, mean_norm, mean_bias = (
        *in_one_piece(
            (partial_query[0], partial_key[0], partial_value[0]),
            (("replica_0", "replica_1"), "replica_2"),
            0,
            1,
        ),
        sum_by_axis(partial_mixed[0], (("replica_0", "replica_1"), "replica_2"), 1),
        sum_by_axis(partial_norm[0], (("replica_0", "replica_1"), "replica_2"), 0),
        sum_by_axis(partial_bias[0], (("replica_0", "replica_1"), "replica_2"), 0),
    )
    mean_rate = lax.axis_size(REPLICA) ** (-0.5)
    mean_query = mean_query * mean_rate
    mean_key = mean_key * mean_rate
    mean_value = mean_value * mean_rate
    mean_mixed = mean_mixed * mean_rate
    mean_norm = mean_norm * mean_rate
    mean_bias = mean_bias * mean_rate
    (
        own_query,
        own_key,
        own_value,
        own_mixed,
        slope_query_norm,
        slope_key_norm,
        slope_value_norm,
        slope_mixed_norm,
    ) = together(
        (
            jnp.sum(master_query * master_query, axis=1, keepdims=True),
            jnp.sum(master_key * master_key, axis=1, keepdims=True),
            jnp.sum(master_value * master_value, axis=1, keepdims=True),
            jnp.sum(master_mixed * master_mixed, axis=0, keepdims=True),
            jnp.sum(mean_query * mean_query, axis=1, keepdims=True),
            jnp.sum(mean_key * mean_key, axis=1, keepdims=True),
            jnp.sum(mean_value * mean_value, axis=1, keepdims=True),
            jnp.sum(mean_mixed * mean_mixed, axis=0, keepdims=True),
        ),
        "model",
    )
    mean_query = mean_query * (jnp.sqrt(own_query) * lax.rsqrt(slope_query_norm + 1e-06))
    mean_key = mean_key * (jnp.sqrt(own_key) * lax.rsqrt(slope_key_norm + 1e-06))
    mean_value = mean_value * (jnp.sqrt(own_value) * lax.rsqrt(slope_value_norm + 1e-06))
    mean_mixed = mean_mixed * (jnp.sqrt(own_mixed) * lax.rsqrt(slope_mixed_norm + 1e-06))
    state_new_query = hold_rate * memory_query + (1.0 - hold_rate) * mean_query * mean_query
    stepped_query = master_query - learn_rate * mean_query * lax.rsqrt(state_new_query + 1e-06)
    state_new_key = hold_rate * memory_key + (1.0 - hold_rate) * mean_key * mean_key
    stepped_key = master_key - learn_rate * mean_key * lax.rsqrt(state_new_key + 1e-06)
    state_new_value = hold_rate * memory_value + (1.0 - hold_rate) * mean_value * mean_value
    stepped_value = master_value - learn_rate * mean_value * lax.rsqrt(state_new_value + 1e-06)
    state_new_mixed = hold_rate * memory_mixed + (1.0 - hold_rate) * mean_mixed * mean_mixed
    stepped_mixed = master_mixed - learn_rate * mean_mixed * lax.rsqrt(state_new_mixed + 1e-06)
    state_new_norm = hold_rate * memory_norm + (1.0 - hold_rate) * mean_norm * mean_norm
    stepped_norm = master_norm - learn_rate * mean_norm * lax.rsqrt(state_new_norm + 1e-06)
    state_new_bias = hold_rate * memory_bias + (1.0 - hold_rate) * mean_bias * mean_bias
    stepped_bias = master_bias - learn_rate * mean_bias * lax.rsqrt(state_new_bias + 1e-06)
    compute_query, compute_key, compute_value, compute_mixed, compute_norm, compute_bias = (
        gather_turned(
            (
                stepped_query.astype(jnp.bfloat16),
                stepped_key.astype(jnp.bfloat16),
                stepped_value.astype(jnp.bfloat16),
                stepped_mixed.astype(jnp.bfloat16),
                stepped_norm.astype(jnp.bfloat16),
                stepped_bias.astype(jnp.bfloat16),
            ),
            REPLICA,
            (0, 0, 0, 1, 0, 0),
        )
    )
    return (
        compute_query,
        compute_key,
        compute_value,
        compute_mixed,
        compute_norm,
        compute_bias,
        stepped_query,
        stepped_key,
        stepped_value,
        stepped_mixed,
        stepped_norm,
        stepped_bias,
        state_new_query,
        state_new_key,
        state_new_value,
        state_new_mixed,
        state_new_norm,
        state_new_bias,
    )


def solution(mesh):
    split = Mesh(
        mesh.devices.reshape(2, 4, 2, mesh.shape["model"]),
        ("replica_0", "replica_1", "replica_2", "model"),
    )
    return jax.shard_map(
        shards,
        mesh=split,
        in_specs=(
            P(REPLICA, None, "model"),
            P(REPLICA, None, "model"),
            P(REPLICA, None, "model"),
            P(REPLICA, "model", None),
            P(REPLICA, None),
            P(REPLICA, None),
            P(REPLICA, "model"),
            P(REPLICA, "model"),
            P(REPLICA, "model"),
            P("model", REPLICA),
            P(REPLICA),
            P(REPLICA),
            P(REPLICA, "model"),
            P(REPLICA, "model"),
            P(REPLICA, "model"),
            P("model", REPLICA),
            P(REPLICA),
            P(REPLICA),
        ),
        out_specs=(
            P(None, "model"),
            P(None, "model"),
            P(None, "model"),
            P("model", None),
            P(),
            P(),
            P(REPLICA, "model"),
            P(REPLICA, "model"),
            P(REPLICA, "model"),
            P("model", REPLICA),
            P(REPLICA),
            P(REPLICA),
            P(REPLICA, "model"),
            P(REPLICA, "model"),
            P(REPLICA, "model"),
            P("model", REPLICA),
            P(REPLICA),
            P(REPLICA),
        ),
        check_vma=False,
    )
```

profile of v0, /device:TPU:1, one launch (start us, length us, event | category | flops | bytes accessed | tf_op | source)
XLA Modules:
  0.0 159.4 jit_solution(13763253603055868574)
XLA Ops:
  7.2 1.3 copy.166
  8.5 6.4 %all-to-all-start.5 = ((f32[2,8,128]{2,1,0:T(8,128)}), f32[2,8,128]{2,1,0:T(8,128)S(1)}, u32[]{:S(2)}, u32[]{:S(2)}) async-start(f32[2,8,128]{2,1,0:T(8,128)} %copy.166), calls=%async_computation.5 | async-start | bytes 16384 | tf_op jit(solution)/shard_map/all_to_all | solution.py:19
  14.9 2.1 %maximum_bitcast_fusion = f32[2,8,128,384]{3,2,0,1:T(8,128)S(1)} fusion(f32[8,2,128,128]{3,2,1,0:T(8,128)} %bitcast.29, f32[8,2,128,128]{3,2,1,0:T(8,128)} %bitcast.30, f32[8,2,128,128]{3,2,1,0:T(8,128)} %bitcast.31), kind=kLoop, calls=%fused_computation | loop fusion | flops 1572864 | bytes 6291456 | tf_op jit(solution)/shard_map/transpose | solution.py:14
  17.0 1.9 %copy.142 = f32[2,8,128,384]{3,2,1,0:T(8,128)} copy(f32[2,8,128,384]{3,2,0,1:T(8,128)S(1)} %maximum_bitcast_fusion) | data formatting | bytes 6291456 | tf_op jit(solution)/shard_map/transpose | solution.py:14
  18.9 0.3 copy.146
  19.2 1.3 copy.147
  20.6 4.0 %all-to-all-start = ((f32[2,8,128,384]{3,2,1,0:T(8,128)}), f32[2,8,128,384]{3,2,1,0:T(8,128)S(1)}, u32[]{:S(2)}, u32[]{:S(2)}) async-start(f32[2,8,128,384]{3,2,1,0:T(8,128)} %copy.142), calls=%async_computation | async-start | bytes 6291456 | tf_op jit(solution)/shard_map/all_to_all | solution.py:19
  24.5 0.6 reduce_sum.166
  25.1 2.7 %all-to-all-done = f32[2,8,128,384]{3,2,1,0:T(8,128)S(1)} async-done(((f32[2,8,128,384]{3,2,1,0:T(8,128)}), f32[2,8,128,384]{3,2,1,0:T(8,128)S(1)}, u32[]{:S(2)}, u32[]{:S(2)}) %all-to-all-start) | async-done | bytes 3145760 | tf_op jit(solution)/shard_map/all_to_all | solution.py:19
  27.8 6.6 %all_to_all.54 = f32[2,8,128,128]{3,1,2,0:T(8,128)} all-to-all(f32[2,8,128,128]{3,1,2,0:T(8,128)} %copy.147), channel_id=1, replica_groups=mesh['replica_0'=2,'replica_1'=4,'replica_2'=2,'model'=16] {'replica_2'}, dimensions={0} | all-to-all | bytes 2097152 | tf_op jit(solution)/shard_map/all_to_all | solution.py:19
  34.3 3.7 %all_to_all.55 = f32[2,8,128]{2,1,0:T(8,128)S(1)} all-to-all(f32[2,8,128]{2,1,0:T(8,128)S(1)} %copy.167), channel_id=1, replica_groups=mesh['replica_0'=2,'replica_1'=4,'replica_2'=2,'model'=16] {'replica_2'}, dimensions={0} | all-to-all | bytes 16384 | tf_op jit(solution)/shard_map/all_to_all | solution.py:19
  38.1 3.8 %all-to-all-start.6 = ((f32[8,1,128]{2,1,0:T(1,128)}), f32[8,1,128]{2,1,0:T(1,128)S(1)}, u32[]{:S(2)}, u32[]{:S(2)}) async-start(f32[8,1,128]{2,1,0:T(1,128)} %bitcast.11), calls=%async_computation.6 | async-start | bytes 8192 | tf_op jit(solution)/shard_map/all_to_all | solution.py:26
  41.9 0.6 reduce_sum.168
  42.5 4.4 %all-to-all-done.6 = f32[8,1,128]{2,1,0:T(1,128)S(1)} async-done(((f32[8,1,128]{2,1,0:T(1,128)}), f32[8,1,128]{2,1,0:T(1,128)S(1)}, u32[]{:S(2)}, u32[]{:S(2)}) %all-to-all-start.6) | async-done | bytes 4128 | tf_op jit(solution)/shard_map/all_to_all | solution.py:26
  46.9 3.3 %all-to-all-start.8 = ((f32[8,1,128]{2,1,0:T(1,128)}), f32[8,1,128]{2,1,0:T(1,128)S(1)}, u32[]{:S(2)}, u32[]{:S(2)}) async-start(f32[8,1,128]{2,1,0:T(1,128)} %bitcast.15), calls=%async_computation.8 | async-start | bytes 8192 | tf_op jit(solution)/shard_map/all_to_all | solution.py:26
  50.2 2.1 %reduce_sum.162 = f32[8,128,128]{2,0,1:T(8,128)} reduce(f32[2,8,128,128]{3,1,2,0:T(8,128)} %all_to_all.54, f32[]{:T(128)} %constant.8.clone.1), dimensions={0}, to_apply=%region_9.0 | reduce | flops 131072 | bytes 1572868 | tf_op jit(solution)/shard_map/reduce_sum | solution.py:20
  52.3 1.9 %copy.149 = f32[8,128,128]{2,1,0:T(8,128)} copy(f32[8,128,128]{2,0,1:T(8,128)} %reduce_sum.162) | data formatting | bytes 1048576 | tf_op jit(solution)/shard_map/reduce_sum | solution.py:20
  54.3 0.8 all-to-all-done.8
  55.1 4.3 %all-to-all-start.3 = ((f32[8,128,128]{2,1,0:T(8,128)}), f32[8,128,128]{2,1,0:T(8,128)}, u32[]{:S(2)}, u32[]{:S(2)}) async-start(f32[8,128,128]{2,1,0:T(8,128)} %copy.149), calls=%async_computation.3 | async-start | bytes 1048576 | tf_op jit(solution)/shard_map/all_to_all | solution.py:26
  59.4 1.5 reduce_sum.153
  60.9 5.7 %all-to-all-done.3 = f32[8,128,128]{2,1,0:T(8,128)} async-done(((f32[8,128,128]{2,1,0:T(8,128)}), f32[8,128,128]{2,1,0:T(8,128)}, u32[]{:S(2)}, u32[]{:S(2)}) %all-to-all-start.3) | async-done | bytes 524320 | tf_op jit(solution)/shard_map/all_to_all | solution.py:26
  66.6 3.6 %all-to-all-start.1 = ((f32[8,128,384]{2,1,0:T(8,128)}), f32[8,128,384]{2,1,0:T(8,128)S(1)}, u32[]{:S(2)}, u32[]{:S(2)}) async-start(f32[8,128,384]{2,1,0:T(8,128)} %reduce_sum.153), calls=%async_computation.1 | async-start | bytes 3145728 | tf_op jit(solution)/shard_map/all_to_all | solution.py:26
  70.2 0.1 copy.157
  70.3 0.1 copy.160
  70.4 0.1 copy.154
  70.5 0.1 copy.155
  70.6 0.1 copy.164
  70.7 0.1 copy.165
  71.0 0.1 copy.153
  71.0 0.1 multiply_reduce_fusion.7
  71.2 0.1 multiply_reduce_fusion.6
  71.3 0.1 multiply_reduce_fusion.5
  71.5 0.5 convert_bitcast_fusion.2
  72.0 0.1 copy.170
  72.2 1.1 reduce_sum.163
  73.3 0.1 copy.150
  73.4 0.1 multiply_reduce_fusion
  73.5 13.5 %all-to-all-done.1 = f32[8,128,384]{2,1,0:T(8,128)S(1)} async-done(((f32[8,128,384]{2,1,0:T(8,128)}), f32[8,128,384]{2,1,0:T(8,128)S(1)}, u32[]{:S(2)}, u32[]{:S(2)}) %all-to-all-start.1) | async-done | bytes 1572896 | tf_op jit(solution)/shard_map/all_to_all | solution.py:26
  87.1 0.1 copy.181
  87.3 0.1 copy.182
  87.4 0.1 copy.145
  87.6 0.7 broadcast_in_dim.3
  88.2 9.9 %all-to-all-start.4 = ((f32[16,1,1024]{2,1,0:T(1,128)}), f32[16,1,1024]{2,1,0:T(1,128)S(1)}, u32[]{:S(2)}, u32[]{:S(2)}) async-start(f32[16,1,1024]{2,1,0:T(1,128)} %broadcast_in_dim.3), calls=%async_computation.4 | async-start | bytes 131072 | tf_op jit(solution)/shard_map/all_to_all | solution.py:38
  98.2 0.5 convert_bitcast_fusion.1
  98.7 0.1 copy.171
  98.8 8.2 %all-to-all-done.4 = f32[16,1,1024]{2,1,0:T(1,128)S(1)} async-done(((f32[16,1,1024]{2,1,0:T(1,128)}), f32[16,1,1024]{2,1,0:T(1,128)S(1)}, u32[]{:S(2)}, u32[]{:S(2)}) %all-to-all-start.4) | async-done | bytes 65568 | tf_op jit(solution)/shard_map/all_to_all | solution.py:38
  107.2 0.1 copy.156
  107.3 0.1 copy.159
  107.4 0.1 copy.162
  107.5 0.1 convert_bitcast_fusion
  107.6 0.1 copy.169
  107.8 0.1 copy.168
  107.9 0.8 fusion.3
  108.7 0.8 concatenate.21
  109.4 0.7 copy.174
  110.2 0.7 copy.175
  110.9 0.7 copy.177
  111.6 0.7 copy.178
  112.4 0.7 copy.173
  113.1 0.7 copy.176
  113.8 32.6 %all-gather.2.cloned.1.call-done = bf16[2048,514]{1,0:T(8,128)(2,1)} async-done(((bf16[128,514]{1,0:T(8,128)(2,1)}), bf16[2048,514]{1,0:T(8,128)(2,1)}) %all-gather.2.cloned.1.call-update) | async-done | bytes 2105360 | tf_op jit(solution)/shard_map/all_gather | solution.py:56
  146.4 2.7 %slice_bitcast_fusion = (bf16[128,2048]{0,1:T(8,128)(2,1)S(1)}, bf16[2048,128]{1,0:T(8,128)(2,1)}, bf16[2048,128]{1,0:T(8,128)(2,1)}, bf16[2048,128]{1,0:T(8,128)(2,1)}) fusion(bf16[2048,514]{1,0:T(8,128)(2,1)} %all-gather.2.cloned.1.call-done), kind=kLoop, calls=%fused_computation.3 | loop fusion | bytes 4194304 | tf_op jit(solution)/shard_map/transpose | solution.py:59
  149.1 1.0 copy.172
  150.1 2.5 %slice_reduce_fusion = (bf16[2048]{0:T(1024)(128)(2,1)}, bf16[2048]{0:T(1024)(128)(2,1)}) fusion(bf16[2048,514]{1,0:T(8,128)(2,1)} %all-gather.2.cloned.1.call-done), kind=kLoop, calls=%fused_computation.1 | loop fusion | bytes 16384 | tf_op jit(solution)/shard_map/slice | solution.py:58
  (56 shorter events, 0.8 us)
Async XLA Ops:
  8.5 12.1 %all-to-all-start.5 = ((f32[2,8,128]{2,1,0:T(8,128)}), f32[2,8,128]{2,1,0:T(8,128)S(1)}, u32[]{:S(2)}, u32[]{:S(2)}) async-start(f32[2,8,128]{2,1,0:T(8,128)} %copy.166), calls=%async_computation.5 | async-start | bytes 16384 | tf_op jit(solution)/shard_map/all_to_all | solution.py:19
  17.0 1.9 %copy-start = (f32[1,128,2048]{2,1,0:T(8,128)S(1)}, f32[1,128,2048]{2,1,0:T(8,128)}, u32[]{:S(2)}) copy-start(f32[1,128,2048]{2,1,0:T(8,128)} %param.21) | copy-start | bytes 3145732
  18.9 1.7 %copy-start.9 = (f32[1,2048]{1,0:T(1,128)S(1)}, f32[1,2048]{1,0:T(1,128)}, u32[]{:S(2)}) copy-start(f32[1,2048]{1,0:T(1,128)} %param.23) | copy-start | bytes 24580
  20.6 7.2 %all-to-all-start = ((f32[2,8,128,384]{3,2,1,0:T(8,128)}), f32[2,8,128,384]{3,2,1,0:T(8,128)S(1)}, u32[]{:S(2)}, u32[]{:S(2)}) async-start(f32[2,8,128,384]{3,2,1,0:T(8,128)} %copy.142), calls=%async_computation | async-start | bytes 6291456 | tf_op jit(solution)/shard_map/all_to_all | solution.py:19
  38.1 8.8 %all-to-all-start.6 = ((f32[8,1,128]{2,1,0:T(1,128)}), f32[8,1,128]{2,1,0:T(1,128)S(1)}, u32[]{:S(2)}, u32[]{:S(2)}) async-start(f32[8,1,128]{2,1,0:T(1,128)} %bitcast.11), calls=%async_computation.6 | async-start | bytes 8192 | tf_op jit(solution)/shard_map/all_to_all | solution.py:26
  46.9 8.2 %all-to-all-start.8 = ((f32[8,1,128]{2,1,0:T(1,128)}), f32[8,1,128]{2,1,0:T(1,128)S(1)}, u32[]{:S(2)}, u32[]{:S(2)}) async-start(f32[8,1,128]{2,1,0:T(1,128)} %bitcast.15), calls=%async_computation.8 | async-start | bytes 8192 | tf_op jit(solution)/shard_map/all_to_all | solution.py:26
  55.1 11.5 %all-to-all-start.3 = ((f32[8,128,128]{2,1,0:T(8,128)}), f32[8,128,128]{2,1,0:T(8,128)}, u32[]{:S(2)}, u32[]{:S(2)}) async-start(f32[8,128,128]{2,1,0:T(8,128)} %copy.149), calls=%async_computation.3 | async-start | bytes 1048576 | tf_op jit(solution)/shard_map/all_to_all | solution.py:26
  59.3 10.9 %copy-start.5 = (f32[128,128]{1,0:T(8,128)S(1)}, f32[128,128]{1,0:T(8,128)}, u32[]{:S(2)}) copy-start(f32[128,128]{1,0:T(8,128)} %param.32) | copy-start | bytes 196612
  59.3 11.1 %copy-start.6 = (f32[128,128]{1,0:T(8,128)S(1)}, f32[128,128]{1,0:T(8,128)}, u32[]{:S(2)}) copy-start(f32[128,128]{1,0:T(8,128)} %param.31) | copy-start | bytes 196612
  59.4 11.2 %copy-start.3 = (f32[128,128]{1,0:T(8,128)S(1)}, f32[128,128]{1,0:T(8,128)}, u32[]{:S(2)}) copy-start(f32[128,128]{1,0:T(8,128)} %param.25) | copy-start | bytes 196612
  59.4 11.3 %copy-start.7 = (f32[128,128]{1,0:T(8,128)S(1)}, f32[128,128]{1,0:T(8,128)}, u32[]{:S(2)}) copy-start(f32[128,128]{1,0:T(8,128)} %param.33) | copy-start | bytes 196612
  60.9 9.8 %copy-start.4 = (f32[128,128]{1,0:T(8,128)S(1)}, f32[128,128]{1,0:T(8,128)}, u32[]{:S(2)}) copy-start(f32[128,128]{1,0:T(8,128)} %param.27) | copy-start | bytes 196612
  60.9 9.9 %copy-start.8 = (f32[128,128]{1,0:T(8,128)S(1)}, f32[128,128]{1,0:T(8,128)}, u32[]{:S(2)}) copy-start(f32[128,128]{1,0:T(8,128)} %param.30) | copy-start | bytes 196612
  60.9 10.1 %copy-start.2 = (f32[128,128]{1,0:T(8,128)S(1)}, f32[128,128]{1,0:T(8,128)}, u32[]{:S(2)}) copy-start(f32[128,128]{1,0:T(8,128)} %param.24) | copy-start | bytes 196612
  60.9 10.4 %copy-start.1 = (f32[128,128]{1,0:T(8,128)S(1)}, f32[128,128]{1,0:T(8,128)}, u32[]{:S(2)}) copy-start(f32[128,128]{1,0:T(8,128)} %param.26) | copy-start | bytes 196612
  60.9 10.6 %copy-start.10 = (f32[128]{0:T(128)S(1)}, f32[128]{0:T(128)}, u32[]{:S(2)}) copy-start(f32[128]{0:T(128)} %param.28) | copy-start | bytes 1540
  60.9 10.6 %copy-start.11 = (f32[128]{0:T(128)S(1)}, f32[128]{0:T(128)}, u32[]{:S(2)}) copy-start(f32[128]{0:T(128)} %param.34) | copy-start | bytes 1540
  66.6 20.4 %all-to-all-start.1 = ((f32[8,128,384]{2,1,0:T(8,128)}), f32[8,128,384]{2,1,0:T(8,128)S(1)}, u32[]{:S(2)}, u32[]{:S(2)}) async-start(f32[8,128,384]{2,1,0:T(8,128)} %reduce_sum.153), calls=%async_computation.1 | async-start | bytes 3145728 | tf_op jit(solution)/shard_map/all_to_all | solution.py:26
  70.2 28.0 %copy-start.12 = (f32[128]{0:T(128)S(1)}, f32[128]{0:T(128)}, u32[]{:S(2)}) copy-start(f32[128]{0:T(128)} %param.29) | copy-start | bytes 1540
  70.2 28.0 %copy-start.13 = (f32[128]{0:T(128)S(1)}, f32[128]{0:T(128)}, u32[]{:S(2)}) copy-start(f32[128]{0:T(128)} %param.35) | copy-start | bytes 1540
  88.2 18.8 %all-to-all-start.4 = ((f32[16,1,1024]{2,1,0:T(1,128)}), f32[16,1,1024]{2,1,0:T(1,128)S(1)}, u32[]{:S(2)}, u32[]{:S(2)}) async-start(f32[16,1,1024]{2,1,0:T(1,128)} %broadcast_in_dim.3), calls=%async_computation.4 | async-start | bytes 131072 | tf_op jit(solution)/shard_map/all_to_all | solution.py:38
  98.1 48.3 %all-gather.2.cloned.1.call-start = ((), (), s32[]{:S(2)}) async-start(), calls=%async_computation.9 | async-start | bytes 2785280 | tf_op jit(solution)/shard_map/all_gather | solution.py:56
Sparse Core Ops, SparseCore 0:
  109.6 36.7 all-gather.1
where the time goes:
time: 160 us; the launch traced here: 159 us
  waiting for transfers between devices  67.8 us (42%)
  starting transfers between devices  35.3 us (22%)
  local copies, waits for them, and re-layouts  20.7 us (13%)
  between operations  14.5 us (9%)
  other arithmetic  10.8 us (7%)
  blocking collectives  10.3 us (6%)
    all_gather x1, waiting for transfers between devices, gather_turned(): out, at, outs = (lax.all_gather(both, axis, axis=0, tiled=True), 0, [])  32.6 us
    all_to_all x4, waiting for transfers between devices, sum_by_axis(): return jnp.sum(lax.all_to_all(own, far, 0, 0, tiled=True), axis=0)  24.4 us
    all_to_all x4, starting transfers between devices, sum_by_axis(): return jnp.sum(lax.all_to_all(own, far, 0, 0, tiled=True), axis=0)  15 us
    all_to_all x2, starting transfers between devices, sum_at_owner(): blocks = lax.all_to_all(cut_along(x, dim, size), axis, 0, 0, tiled=True)  10.4 us
    all_to_all x2, blocking collectives, sum_at_owner(): blocks = lax.all_to_all(cut_along(x, dim, size), axis, 0, 0, tiled=True)  10.3 us
    all_to_all x1, starting transfers between devices, copy_for_each(): return lax.all_to_all(copies, axis, split_axis=0, concat_axis=0, tiled=True)  9.85 us
    all_to_all x1, waiting for transfers between devices, copy_for_each(): return lax.all_to_all(copies, axis, split_axis=0, concat_axis=0, tiled=True)  8.2 us
    unnamed x52, local copies, waits for them, and re-layouts  6.61 us
  transfers between devices with their start and end apart: 8, of which 7 were waited for; matrix products, arithmetic and copies ran while one was open for 13% of the time, Pallas kernels for 0%

commit v1 on v0

--- a/solution.py
+++ b/solution.py
@@ -7,6 +7,13 @@
 REPLICA = ("replica_0", "replica_1", "replica_2")
 learn_rate = 0.015
 hold_rate = 0.8
+
+
+def exchange_gather(x, name, dim):
+    size = lax.axis_size(name)
+    parts = jnp.stack([x for _ in range(size)])
+    parts = lax.all_to_all(parts, name, split_axis=0, concat_axis=0)
+    return jnp.concatenate(parts, axis=dim)
 
 
 def cut_along(x, dim, size):
@@ -53,7 +60,7 @@
 def gather_turned(arrays, axis, dims):
     turned = [jnp.moveaxis(a, dim, 0) for a, dim in zip(arrays, dims)]
     both = jnp.concatenate([t.reshape(len(t), -1) for t in turned], axis=1)
-    out, at, outs = (lax.all_gather(both, axis, axis=0, tiled=True), 0, [])
+    out, at, outs = (exchange_gather(both, axis, 0), 0, [])
     for t, dim in zip(turned, dims):
         share = out[:, at : at + t[0].size].reshape(-1, *t.shape[1:])
         outs.append(jnp.moveaxis(share, 0, dim))

time: 160 us -> 149 us (0.931)
  between operations: 14.5 us -> 1.17 us
  starting transfers between devices: 35.3 us -> 44.7 us
  waiting for transfers between devices: 67.8 us -> 58.9 us
    all_gather x1 -> x0, waiting for transfers between devices: 32.6 us -> none  [gather_turned(): out, at, outs = (lax.all_gather(both, axis, axis=0, tiled=True), 0, [])]
    all_to_all x0 -> x1, waiting for transfers between devices: none -> 23.7 us  [exchange_gather(): parts = lax.all_to_all(parts, name, split_axis=0, concat_axis=0)]
    all_to_all x0 -> x1, starting transfers between devices: none -> 9.45 us  [exchange_gather(): parts = lax.all_to_all(parts, name, split_axis=0, concat_axis=0)]
    unnamed x52 -> x56, local copies, waits for them, and re-layouts: 6.61 us -> 9.52 us
    slice x1, local copies, waits for them, and re-layouts: 2.46 us -> 0.64 us  [gather_turned(): share = out[:, at:at + t[0].size].reshape(-1, *t.shape[1:])]
    transpose x1, local copies, waits for them, and re-layouts: 2.74 us -> 1.01 us  [gather_turned(): outs.append(jnp.moveaxis(share, 0, dim))]
    another operation x0 -> x1, local copies, waits for them, and re-layouts: none -> 1.63 us  [exchange_gather(): parts = jnp.stack([x for _ in range(size)])]
  transfers between devices with their start and end apart: 8 -> 8, of which waited for: 7 -> 7; matrix products, arithmetic and copies ran while one was open for 13% -> 14% of each run, Pallas kernels for 0% -> 0%
where the time goes in v1:
time: 149 us; the launch traced here: 147 us
  waiting for transfers between devices  58.9 us (40%)
  starting transfers between devices  44.7 us (30%)
  local copies, waits for them, and re-layouts  21.5 us (14%)
  other arithmetic  10.8 us (7%)
  blocking collectives  10.3 us (7%)
    all_to_all x4, waiting for transfers between devices, sum_by_axis(): return jnp.sum(lax.all_to_all(own, far, 0, 0, tiled=True), axis=0)  24.4 us
    all_to_all x1, waiting for transfers between devices, exchange_gather(): parts = lax.all_to_all(parts, name, split_axis=0, concat_axis=0)  23.7 us
    all_to_all x4, starting transfers between devices, sum_by_axis(): return jnp.sum(lax.all_to_all(own, far, 0, 0, tiled=True), axis=0)  15 us
    all_to_all x2, starting transfers between devices, sum_at_owner(): blocks = lax.all_to_all(cut_along(x, dim, size), axis, 0, 0, tiled=True)  10.4 us
    all_to_all x2, blocking collectives, sum_at_owner(): blocks = lax.all_to_all(cut_along(x, dim, size), axis, 0, 0, tiled=True)  10.3 us
    all_to_all x1, starting transfers between devices, copy_for_each(): return lax.all_to_all(copies, axis, split_axis=0, concat_axis=0, tiled=True)  9.85 us
    unnamed x56, local copies, waits for them, and re-layouts  9.52 us
    all_to_all x1, starting transfers between devices, exchange_gather(): parts = lax.all_to_all(parts, name, split_axis=0, concat_axis=0)  9.45 us
  transfers between devices with their start and end apart: 8, of which 7 were waited for; matrix products, arithmetic and copies ran while one was open for 14% of the time, Pallas kernels for 0%

profile of v1, /device:TPU:1, one launch (start us, length us, event | category | flops | bytes accessed | tf_op | source)
XLA Modules:
  0.0 147.4 jit_solution(17260735549495999148)
XLA Ops:
  0.7 1.3 copy.138
  2.0 6.4 %all-to-all-start.5 = ((f32[2,8,128]{2,1,0:T(8,128)}), f32[2,8,128]{2,1,0:T(8,128)S(1)}, u32[]{:S(2)}, u32[]{:S(2)}) async-start(f32[2,8,128]{2,1,0:T(8,128)} %copy.138), calls=%async_computation.5 | async-start | bytes 16384 | tf_op jit(solution)/shard_map/all_to_all | solution.py:26
  8.4 2.1 %maximum_bitcast_fusion = f32[2,8,128,384]{3,2,0,1:T(8,128)S(1)} fusion(f32[8,2,128,128]{3,2,1,0:T(8,128)} %bitcast.40, f32[8,2,128,128]{3,2,1,0:T(8,128)} %bitcast.41, f32[8,2,128,128]{3,2,1,0:T(8,128)} %bitcast.42), kind=kLoop, calls=%fused_computation | loop fusion | flops 1572864 | bytes 6291456 | tf_op jit(solution)/shard_map/transpose | solution.py:21
  10.5 1.9 %copy.114 = f32[2,8,128,384]{3,2,1,0:T(8,128)} copy(f32[2,8,128,384]{3,2,0,1:T(8,128)S(1)} %maximum_bitcast_fusion) | data formatting | bytes 6291456 | tf_op jit(solution)/shard_map/transpose | solution.py:21
  12.4 0.3 copy.118
  12.7 1.3 copy.119
  14.0 4.0 %all-to-all-start = ((f32[2,8,128,384]{3,2,1,0:T(8,128)}), f32[2,8,128,384]{3,2,1,0:T(8,128)S(1)}, u32[]{:S(2)}, u32[]{:S(2)}) async-start(f32[2,8,128,384]{3,2,1,0:T(8,128)} %copy.114), calls=%async_computation | async-start | bytes 6291456 | tf_op jit(solution)/shard_map/all_to_all | solution.py:26
  18.0 0.6 reduce_sum.166
  18.6 2.7 %all-to-all-done = f32[2,8,128,384]{3,2,1,0:T(8,128)S(1)} async-done(((f32[2,8,128,384]{3,2,1,0:T(8,128)}), f32[2,8,128,384]{3,2,1,0:T(8,128)S(1)}, u32[]{:S(2)}, u32[]{:S(2)}) %all-to-all-start) | async-done | bytes 3145760 | tf_op jit(solution)/shard_map/all_to_all | solution.py:26
  21.2 6.6 %all_to_all.59 = f32[2,8,128,128]{3,1,2,0:T(8,128)} all-to-all(f32[2,8,128,128]{3,1,2,0:T(8,128)} %copy.119), channel_id=1, replica_groups=mesh['replica_0'=2,'replica_1'=4,'replica_2'=2,'model'=16] {'replica_2'}, dimensions={0} | all-to-all | bytes 2097152 | tf_op jit(solution)/shard_map/all_to_all | solution.py:26
  27.8 3.7 %all_to_all.60 = f32[2,8,128]{2,1,0:T(8,128)S(1)} all-to-all(f32[2,8,128]{2,1,0:T(8,128)S(1)} %copy.139), channel_id=1, replica_groups=mesh['replica_0'=2,'replica_1'=4,'replica_2'=2,'model'=16] {'replica_2'}, dimensions={0} | all-to-all | bytes 16384 | tf_op jit(solution)/shard_map/all_to_all | solution.py:26
  31.5 3.8 %all-to-all-start.6 = ((f32[8,1,128]{2,1,0:T(1,128)}), f32[8,1,128]{2,1,0:T(1,128)S(1)}, u32[]{:S(2)}, u32[]{:S(2)}) async-start(f32[8,1,128]{2,1,0:T(1,128)} %bitcast.11), calls=%async_computation.6 | async-start | bytes 8192 | tf_op jit(solution)/shard_map/all_to_all | solution.py:33
  35.4 0.6 reduce_sum.168
  36.0 4.4 %all-to-all-done.6 = f32[8,1,128]{2,1,0:T(1,128)S(1)} async-done(((f32[8,1,128]{2,1,0:T(1,128)}), f32[8,1,128]{2,1,0:T(1,128)S(1)}, u32[]{:S(2)}, u32[]{:S(2)}) %all-to-all-start.6) | async-done | bytes 4128 | tf_op jit(solution)/shard_map/all_to_all | solution.py:33
  40.3 3.3 %all-to-all-start.8 = ((f32[8,1,128]{2,1,0:T(1,128)}), f32[8,1,128]{2,1,0:T(1,128)S(1)}, u32[]{:S(2)}, u32[]{:S(2)}) async-start(f32[8,1,128]{2,1,0:T(1,128)} %bitcast.15), calls=%async_computation.8 | async-start | bytes 8192 | tf_op jit(solution)/shard_map/all_to_all | solution.py:33
  43.7 2.1 %reduce_sum.162 = f32[8,128,128]{2,0,1:T(8,128)} reduce(f32[2,8,128,128]{3,1,2,0:T(8,128)} %all_to_all.59, f32[]{:T(128)} %constant.8.clone.1), dimensions={0}, to_apply=%region_9.0 | reduce | flops 131072 | bytes 1572868 | tf_op jit(solution)/shard_map/reduce_sum | solution.py:27
  45.8 1.9 %copy.121 = f32[8,128,128]{2,1,0:T(8,128)} copy(f32[8,128,128]{2,0,1:T(8,128)} %reduce_sum.162) | data formatting | bytes 1048576 | tf_op jit(solution)/shard_map/reduce_sum | solution.py:27
  47.7 0.8 all-to-all-done.8
  48.5 4.3 %all-to-all-start.3 = ((f32[8,128,128]{2,1,0:T(8,128)}), f32[8,128,128]{2,1,0:T(8,128)}, u32[]{:S(2)}, u32[]{:S(2)}) async-start(f32[8,128,128]{2,1,0:T(8,128)} %copy.121), calls=%async_computation.3 | async-start | bytes 1048576 | tf_op jit(solution)/shard_map/all_to_all | solution.py:33
  52.8 1.5 %reduce_sum.153 = f32[8,128,384]{2,1,0:T(8,128)} reduce(f32[2,8,128,384]{3,2,1,0:T(8,128)S(1)} %all-to-all-done, f32[]{:T(128)} %constant.8.clone.1), dimensions={0}, to_apply=%region_0.0 | reduce | flops 393216 | bytes 4718596 | tf_op jit(solution)/shard_map/reduce_sum | solution.py:27
  54.4 5.7 %all-to-all-done.3 = f32[8,128,128]{2,1,0:T(8,128)} async-done(((f32[8,128,128]{2,1,0:T(8,128)}), f32[8,128,128]{2,1,0:T(8,128)}, u32[]{:S(2)}, u32[]{:S(2)}) %all-to-all-start.3) | async-done | bytes 524320 | tf_op jit(solution)/shard_map/all_to_all | solution.py:33
  60.0 3.6 %all-to-all-start.1 = ((f32[8,128,384]{2,1,0:T(8,128)}), f32[8,128,384]{2,1,0:T(8,128)S(1)}, u32[]{:S(2)}, u32[]{:S(2)}) async-start(f32[8,128,384]{2,1,0:T(8,128)} %reduce_sum.153), calls=%async_computation.1 | async-start | bytes 3145728 | tf_op jit(solution)/shard_map/all_to_all | solution.py:33
  63.6 0.1 copy.129
  63.8 0.1 copy.132
  64.5 0.1 multiply_reduce_fusion.7
  64.6 0.1 multiply_reduce_fusion.6
  64.8 0.1 multiply_reduce_fusion.5
  65.0 0.5 convert_bitcast_fusion.2
  65.5 0.1 copy.142
  65.7 1.1 reduce_sum.163
  66.8 0.1 multiply_reduce_fusion
  67.0 13.5 %all-to-all-done.1 = f32[8,128,384]{2,1,0:T(8,128)S(1)} async-done(((f32[8,128,384]{2,1,0:T(8,128)}), f32[8,128,384]{2,1,0:T(8,128)S(1)}, u32[]{:S(2)}, u32[]{:S(2)}) %all-to-all-start.1) | async-done | bytes 1572896 | tf_op jit(solution)/shard_map/all_to_all | solution.py:33
  80.7 0.1 copy.158
  80.9 0.1 copy.117
  81.0 0.7 broadcast_in_dim.3
  81.7 9.9 %all-to-all-start.4 = ((f32[16,1,1024]{2,1,0:T(1,128)}), f32[16,1,1024]{2,1,0:T(1,128)S(1)}, u32[]{:S(2)}, u32[]{:S(2)}) async-start(f32[16,1,1024]{2,1,0:T(1,128)} %broadcast_in_dim.3), calls=%async_computation.4 | async-start | bytes 131072 | tf_op jit(solution)/shard_map/all_to_all | solution.py:45
  91.6 0.5 convert_bitcast_fusion.1
  92.1 0.1 copy.143
  92.3 8.3 %all-to-all-done.4 = f32[16,1,1024]{2,1,0:T(1,128)S(1)} async-done(((f32[16,1,1024]{2,1,0:T(1,128)}), f32[16,1,1024]{2,1,0:T(1,128)S(1)}, u32[]{:S(2)}, u32[]{:S(2)}) %all-to-all-start.4) | async-done | bytes 65568 | tf_op jit(solution)/shard_map/all_to_all | solution.py:45
  100.7 0.1 copy.128
  100.9 0.1 copy.134
  101.0 0.1 convert_bitcast_fusion
  101.1 0.1 copy.141
  101.3 0.1 copy.140
  101.4 0.8 fusion.3
  102.1 0.1 concatenate.21
  102.2 0.1 copy.144
  102.4 1.6 %stack.2 = bf16[16,128,514]{1,2,0:T(8,128)(2,1)} broadcast(bf16[128,514]{0,1:T(8,128)(2,1)S(1)} %copy.144), dimensions={1,2} | broadcast | bytes 2236928 | tf_op jit(solution)/shard_map/stack | solution.py:14
  104.0 9.5 %all-to-all-start.9 = ((bf16[16,128,514]{1,2,0:T(8,128)(2,1)}), bf16[16,128,514]{1,2,0:T(8,128)(2,1)S(1)}, u32[]{:S(2)}, u32[]{:S(2)}) async-start(bf16[16,128,514]{1,2,0:T(8,128)(2,1)} %stack.2), calls=%async_computation.9 | async-start | bytes 4259840 | tf_op jit(solution)/shard_map/all_to_all | solution.py:15
  113.4 0.7 copy.150
  114.2 0.7 copy.151
  114.9 0.7 copy.153
  115.6 0.7 copy.154
  116.4 0.7 copy.149
  117.1 0.7 copy.152
  117.8 23.7 %all-to-all-done.9 = bf16[16,128,514]{1,2,0:T(8,128)(2,1)S(1)} async-done(((bf16[16,128,514]{1,2,0:T(8,128)(2,1)}), bf16[16,128,514]{1,2,0:T(8,128)(2,1)S(1)}, u32[]{:S(2)}, u32[]{:S(2)}) %all-to-all-start.9) | async-done | bytes 2105376 | tf_op jit(solution)/shard_map/all_to_all | solution.py:15
  141.5 0.3 copy.169
  141.8 0.4 pad.3
  142.2 0.6 copy.167
  142.7 1.0 slice_bitcast_fusion
  143.7 0.6 slice_reduce_fusion
  144.4 1.0 copy.146
  145.4 1.0 copy.147
  146.4 1.0 copy.148
  (62 shorter events, 1.4 us)
Async XLA Ops:
  2.0 12.1 %all-to-all-start.5 = ((f32[2,8,128]{2,1,0:T(8,128)}), f32[2,8,128]{2,1,0:T(8,128)S(1)}, u32[]{:S(2)}, u32[]{:S(2)}) async-start(f32[2,8,128]{2,1,0:T(8,128)} %copy.138), calls=%async_computation.5 | async-start | bytes 16384 | tf_op jit(solution)/shard_map/all_to_all | solution.py:26
  10.5 1.9 %copy-start = (f32[1,128,2048]{2,1,0:T(8,128)S(1)}, f32[1,128,2048]{2,1,0:T(8,128)}, u32[]{:S(2)}) copy-start(f32[1,128,2048]{2,1,0:T(8,128)} %param.21) | copy-start | bytes 3145732
  12.4 1.7 %copy-start.9 = (f32[1,2048]{1,0:T(1,128)S(1)}, f32[1,2048]{1,0:T(1,128)}, u32[]{:S(2)}) copy-start(f32[1,2048]{1,0:T(1,128)} %param.23) | copy-start | bytes 24580
  14.0 7.2 %all-to-all-start = ((f32[2,8,128,384]{3,2,1,0:T(8,128)}), f32[2,8,128,384]{3,2,1,0:T(8,128)S(1)}, u32[]{:S(2)}, u32[]{:S(2)}) async-start(f32[2,8,128,384]{3,2,1,0:T(8,128)} %copy.114), calls=%async_computation | async-start | bytes 6291456 | tf_op jit(solution)/shard_map/all_to_all | solution.py:26
  31.5 8.8 %all-to-all-start.6 = ((f32[8,1,128]{2,1,0:T(1,128)}), f32[8,1,128]{2,1,0:T(1,128)S(1)}, u32[]{:S(2)}, u32[]{:S(2)}) async-start(f32[8,1,128]{2,1,0:T(1,128)} %bitcast.11), calls=%async_computation.6 | async-start | bytes 8192 | tf_op jit(solution)/shard_map/all_to_all | solution.py:33
  40.3 8.2 %all-to-all-start.8 = ((f32[8,1,128]{2,1,0:T(1,128)}), f32[8,1,128]{2,1,0:T(1,128)S(1)}, u32[]{:S(2)}, u32[]{:S(2)}) async-start(f32[8,1,128]{2,1,0:T(1,128)} %bitcast.15), calls=%async_computation.8 | async-start | bytes 8192 | tf_op jit(solution)/shard_map/all_to_all | solution.py:33
  48.5 11.5 %all-to-all-start.3 = ((f32[8,128,128]{2,1,0:T(8,128)}), f32[8,128,128]{2,1,0:T(8,128)}, u32[]{:S(2)}, u32[]{:S(2)}) async-start(f32[8,128,128]{2,1,0:T(8,128)} %copy.121), calls=%async_computation.3 | async-start | bytes 1048576 | tf_op jit(solution)/shard_map/all_to_all | solution.py:33
  54.3 9.3 %copy-start.5 = (f32[128,128]{1,0:T(8,128)S(1)}, f32[128,128]{1,0:T(8,128)}, u32[]{:S(2)}) copy-start(f32[128,128]{1,0:T(8,128)} %param.32) | copy-start | bytes 196612
  54.3 9.5 %copy-start.6 = (f32[128,128]{1,0:T(8,128)S(1)}, f32[128,128]{1,0:T(8,128)}, u32[]{:S(2)}) copy-start(f32[128,128]{1,0:T(8,128)} %param.31) | copy-start | bytes 196612
  54.3 9.6 %copy-start.3 = (f32[128,128]{1,0:T(8,128)S(1)}, f32[128,128]{1,0:T(8,128)}, u32[]{:S(2)}) copy-start(f32[128,128]{1,0:T(8,128)} %param.25) | copy-start | bytes 196612
  54.3 9.8 %copy-start.7 = (f32[128,128]{1,0:T(8,128)S(1)}, f32[128,128]{1,0:T(8,128)}, u32[]{:S(2)}) copy-start(f32[128,128]{1,0:T(8,128)} %param.33) | copy-start | bytes 196612
  54.3 9.9 %copy-start.4 = (f32[128,128]{1,0:T(8,128)S(1)}, f32[128,128]{1,0:T(8,128)}, u32[]{:S(2)}) copy-start(f32[128,128]{1,0:T(8,128)} %param.27) | copy-start | bytes 196612
  54.3 10.0 %copy-start.8 = (f32[128,128]{1,0:T(8,128)S(1)}, f32[128,128]{1,0:T(8,128)}, u32[]{:S(2)}) copy-start(f32[128,128]{1,0:T(8,128)} %param.30) | copy-start | bytes 196612
  54.3 10.0 %copy-start.2 = (f32[128,128]{1,0:T(8,128)S(1)}, f32[128,128]{1,0:T(8,128)}, u32[]{:S(2)}) copy-start(f32[128,128]{1,0:T(8,128)} %param.24) | copy-start | bytes 196612
  54.4 10.4 %copy-start.1 = (f32[128,128]{1,0:T(8,128)S(1)}, f32[128,128]{1,0:T(8,128)}, u32[]{:S(2)}) copy-start(f32[128,128]{1,0:T(8,128)} %param.26) | copy-start | bytes 196612
  54.4 10.6 %copy-start.10 = (f32[128]{0:T(128)S(1)}, f32[128]{0:T(128)}, u32[]{:S(2)}) copy-start(f32[128]{0:T(128)} %param.28) | copy-start | bytes 1540
  54.4 10.6 %copy-start.11 = (f32[128]{0:T(128)S(1)}, f32[128]{0:T(128)}, u32[]{:S(2)}) copy-start(f32[128]{0:T(128)} %param.34) | copy-start | bytes 1540
  60.0 20.4 %all-to-all-start.1 = ((f32[8,128,384]{2,1,0:T(8,128)}), f32[8,128,384]{2,1,0:T(8,128)S(1)}, u32[]{:S(2)}, u32[]{:S(2)}) async-start(f32[8,128,384]{2,1,0:T(8,128)} %reduce_sum.153), calls=%async_computation.1 | async-start | bytes 3145728 | tf_op jit(solution)/shard_map/all_to_all | solution.py:33
  64.4 27.2 %copy-start.12 = (f32[128]{0:T(128)S(1)}, f32[128]{0:T(128)}, u32[]{:S(2)}) copy-start(f32[128]{0:T(128)} %param.29) | copy-start | bytes 1540
  64.4 27.2 %copy-start.13 = (f32[128]{0:T(128)S(1)}, f32[128]{0:T(128)}, u32[]{:S(2)}) copy-start(f32[128]{0:T(128)} %param.35) | copy-start | bytes 1540
  81.7 18.8 %all-to-all-start.4 = ((f32[16,1,1024]{2,1,0:T(1,128)}), f32[16,1,1024]{2,1,0:T(1,128)S(1)}, u32[]{:S(2)}, u32[]{:S(2)}) async-start(f32[16,1,1024]{2,1,0:T(1,128)} %broadcast_in_dim.3), calls=%async_computation.4 | async-start | bytes 131072 | tf_op jit(solution)/shard_map/all_to_all | solution.py:45
  104.0 37.5 %all-to-all-start.9 = ((bf16[16,128,514]{1,2,0:T(8,128)(2,1)}), bf16[16,128,514]{1,2,0:T(8,128)(2,1)S(1)}, u32[]{:S(2)}, u32[]{:S(2)}) async-start(bf16[16,128,514]{1,2,0:T(8,128)(2,1)} %stack.2), calls=%async_computation.9 | async-start | bytes 4259840 | tf_op jit(solution)/shard_map/all_to_all | solution.py:15
